TPU v7x, 32 devices: a whole 2x2x4 slice. The times are simulated.
32 devices in a mesh: rows: 4 (over z), width: 4 (over y, x), site: 2 (over core).
Axes of the slice: x: 2, y: 2, z: 4, core: 2. Of those that a mesh axis runs over, the one named last changes fastest.
Arguments:
- weight_query: float32 [8192, 4096], P(('site', 'rows'), 'width'), parts along dimension 0, may hold values from -0.125 to 0.125
- moment_query: float32 [8192, 4096], P(('site', 'rows'), 'width'), parts along dimension 0, may hold values from -6 to 6
- square_query: float32 [8192, 4096], P(('site', 'rows'), 'width'), parts along dimension 0, may hold values from 0.1 to 10
- weight_key: float32 [8192, 1024], P(('site', 'rows'), 'width'), parts along dimension 0, may hold values from -0.125 to 0.125
- moment_key: float32 [8192, 1024], P(('site', 'rows'), 'width'), parts along dimension 0, may hold values from -6 to 6
- square_key: float32 [8192, 1024], P(('site', 'rows'), 'width'), parts along dimension 0, may hold values from 0.1 to 10
- weight_value: float32 [8192, 1024], P(('site', 'rows'), 'width'), parts along dimension 0, may hold values from -0.125 to 0.125
- moment_value: float32 [8192, 1024], P(('site', 'rows'), 'width'), parts along dimension 0, may hold values from -6 to 6
- square_value: float32 [8192, 1024], P(('site', 'rows'), 'width'), parts along dimension 0, may hold values from 0.1 to 10
- norm_train: float32 [8192], P(('site', 'rows', 'width')), parts along dimension 0, may hold values from 0.25 to 1.75
- norm_step: float32 [8192], P(('site', 'rows', 'width')), parts along dimension 0, may hold values from -0.3 to 0.3
Outputs:
- final_query: bfloat16 [8192, 4096], P('site', 'width'), parts along dimension 0
- final_key: bfloat16 [8192, 1024], P('site', 'width'), parts along dimension 0
- final_value: bfloat16 [8192, 1024], P('site', 'width'), parts along dimension 0
- column_query: float32 [8192], P(('site', 'width')), parts along dimension 0
- column_key: float32 [2048], P(('site', 'width')), parts along dimension 0
- column_value: float32 [2048], P(('site', 'width')), parts along dimension 0
- serve_norm: bfloat16 [8192], P('site'), parts along dimension 0
- result_query: float32 [8192, 4096], P(('site', 'rows'), 'width'), parts along dimension 0
- result_key: float32 [8192, 1024], P(('site', 'rows'), 'width'), parts along dimension 0
- result_value: float32 [8192, 1024], P(('site', 'rows'), 'width'), parts along dimension 0
There are 2 independent parts, one for each index of `site`. A program takes and returns all parts, laid end to end along the dimension named above; each array names one. Nothing has to cross between parts.
All inputs are finite; a program needn't handle non-finite values.
Results may differ from a plain program's by a relative error of at most 0.001.
Values may be sent and summed in bfloat16 or wider, within the bound.
A program may use at most 128 MiB of HBM per device.

v0:
```python
import jax
import jax.numpy as jnp
from jax import lax
from jax.sharding import PartitionSpec as P

learn_rate = 0.02
decay_rate = 0.05
tiny_value = 1e-08


def per_device(
    weight_query,
    moment_query,
    square_query,
    weight_key,
    moment_key,
    square_key,
    weight_value,
    moment_value,
    square_value,
    norm_train,
    norm_step,
):
    result_query = weight_query - learn_rate * (
        moment_query / (jnp.sqrt(square_query) + tiny_value) + decay_rate * weight_query
    )
    result_key = weight_key - learn_rate * (
        moment_key / (jnp.sqrt(square_key) + tiny_value) + decay_rate * weight_key
    )
    result_value = weight_value - learn_rate * (
        moment_value / (jnp.sqrt(square_value) + tiny_value) + decay_rate * weight_value
    )
    total_query, total_key, total_value = lax.psum(
        (
            jnp.sum(result_query * result_query, axis=0),
            jnp.sum(result_key * result_key, axis=0),
            jnp.sum(result_value * result_value, axis=0),
        ),
        "rows",
    )
    column_query = jnp.sqrt(total_query)
    column_key = jnp.sqrt(total_key)
    column_value = jnp.sqrt(total_value)
    narrow_query, narrow_key, narrow_value = (
        (result_query / column_query).astype(jnp.bfloat16),
        (result_key / column_key).astype(jnp.bfloat16),
        (result_value / column_value).astype(jnp.bfloat16),
    )
    final_query, final_key, final_value = (
        lax.all_gather(narrow_query, "rows", axis=0, tiled=True),
        lax.all_gather(narrow_key, "rows", axis=0, tiled=True),
        lax.all_gather(narrow_value, "rows", axis=0, tiled=True),
    )
    serve_norm = lax.all_gather(
        (norm_train + norm_step).astype(jnp.bfloat16), ("rows", "width"), axis=0, tiled=True
    )
    return (
        final_query,
        final_key,
        final_value,
        column_query,
        column_key,
        column_value,
        serve_norm,
        result_query,
        result_key,
        result_value,
    )


def solution(mesh):
    return jax.shard_map(
        per_device,
        mesh=mesh,
        in_specs=(
            P(("site", "rows"), "width"),
            P(("site", "rows"), "width"),
            P(("site", "rows"), "width"),
            P(("site", "rows"), "width"),
            P(("site", "rows"), "width"),
            P(("site", "rows"), "width"),
            P(("site", "rows"), "width"),
            P(("site", "rows"), "width"),
            P(("site", "rows"), "width"),
            P(("site", "rows", "width")),
            P(("site", "rows", "width")),
        ),
        out_specs=(
            P("site", "width"),
            P("site", "width"),
            P("site", "width"),
            P(("site", "width")),
            P(("site", "width")),
            P(("site", "width")),
            P("site"),
            P(("site", "rows"), "width"),
            P(("site", "rows"), "width"),
            P(("site", "rows"), "width"),
        ),
        check_vma=False,
    )
```

profile of v0, /device:TPU:0, one launch (start us, length us, event | category | flops | bytes accessed | tf_op | source)
XLA Modules:
  0.0 291.6 jit_solution(14504673865674810537)
XLA Ops:
  7.2 0.0 all-gather.7.cloned.1.call-start
  7.3 9.0 %multiply_reduce_fusion = (f32[1024]{0:T(1024)S(1)}, f32[1024,1024]{1,0:T(8,128)}) fusion(f32[1024,1024]{1,0:T(8,128)} %param.11, f32[1024,1024]{1,0:T(8,128)} %param.12, f32[1024,1024]{1,0:T(8,128)} %param.13), kind=kLoop, calls=%fused_computation.1 | loop fusion | flops 8387584 | bytes 16781312 | tf_op jit(solution)/shard_map/reduce_sum | solution.py:35
  16.3 1.1 multiply_reduce_fusion.1
  17.4 0.0 copy-start
  17.5 0.0 copy-start.1
  17.5 13.7 %all-reduce = (f32[1024]{0:T(1024)S(1)}, f32[256]{0:T(256)S(1)}, f32[256]{0:T(256)S(1)}) all-reduce(f32[1024]{0:T(1024)S(1)} %get-tuple-element.17, f32[256]{0:T(256)S(1)} %get-tuple-element.19, f32[256]{0:T(256)S(1)} %get-tuple-element.13), channel_id=1, replica_groups=mesh['rows'=4,'width'=4,'site'=2] {'rows'}, use_global_device_ids=true, to_apply=%region_1.0 | all-reduce | flops 1536 | bytes 12288 | tf_op jit(solution)/shard_map/psum | solution.py:33
  31.2 0.0 copy-start.11
  31.2 0.9 divide_convert_fusion.2
  32.1 0.0 all-gather.7.cloned.1.call-update
  32.1 0.0 all-gather.9.cloned.1.call-start
  32.2 0.0 copy-start.12
  32.2 0.9 divide_convert_fusion.1
  33.1 0.0 all-gather.9.cloned.1.call-update
  33.1 0.0 all-gather.5.cloned.1.call-start
  33.2 4.1 %divide_convert_fusion = bf16[1024,1024]{1,0:T(8,128)(2,1)} fusion(f32[1024,1024]{1,0:T(8,128)} %get-tuple-element.38, f32[1024]{0:T(1024)S(1)} %sqrt.19), kind=kLoop, calls=%fused_computation | loop fusion | flops 2097152 | bytes 6295552 | tf_op jit(solution)/shard_map/convert_element_type | solution.py:45
  37.3 0.0 all-gather.5.cloned.1.call-update
  37.4 38.9 %all-gather = bf16[16,1,256]{2,1,0:T(2,128)(2,1)S(1)} all-gather(bf16[1,1,256]{2,1,0:T(2,128)(2,1)S(1)} %reshape.23), channel_id=1, replica_groups=mesh['rows'=4,'width'=4,'site'=2] {'rows','width'}, dimensions={0}, use_global_device_ids=true | all-gather | bytes 8704 | tf_op jit(solution)/shard_map/all_gather | solution.py:54
  76.4 0.6 copy.21
  77.0 46.0 %all-gather.9.cloned.1.call-done = bf16[4096,256]{1,0:T(8,128)(2,1)} async-done(((bf16[1024,256]{1,0:T(8,128)(2,1)}), bf16[4096,256]{1,0:T(8,128)(2,1)}) %all-gather.9.cloned.1.call-update) | async-done | bytes 2097168 | tf_op jit(solution)/shard_map/all_gather | solution.py:52
  122.9 150.6 %all-gather.5.cloned.1.call-done = bf16[4096,1024]{1,0:T(8,128)(2,1)} async-done(((bf16[1024,1024]{1,0:T(8,128)(2,1)}), bf16[4096,1024]{1,0:T(8,128)(2,1)}) %all-gather.5.cloned.1.call-update) | async-done | bytes 8388624 | tf_op jit(solution)/shard_map/all_gather | solution.py:50
  273.5 7.9 %copy.25 = bf16[4096,1024]{1,0:T(8,128)(2,1)} copy(bf16[4096,1024]{1,0:T(8,128)(2,1)} %all-gather.5.cloned.1.call-done) | data formatting | bytes 16777216
  281.4 1.3 copy.26
  282.8 1.0 copy-done.3
  283.8 1.3 copy.27
  (32 shorter events, 0.1 us)
Async XLA Ops:
  7.2 9.1 %copy-start.4 = (f32[1024,256]{1,0:T(8,128)S(1)}, f32[1024,256]{1,0:T(8,128)}, u32[]{:S(2)}) copy-start(f32[1024,256]{1,0:T(8,128)} %param.17) | copy-start | bytes 3145732
  7.2 69.8 %all-gather.7.cloned.1.call-start = ((), (), s32[]{:S(2)}) async-start(), calls=%async_computation.1 | async-start | bytes 2621440 | tf_op jit(solution)/shard_map/all_gather | solution.py:51
  7.2 9.0 %copy-start.5 = (f32[1024,256]{1,0:T(8,128)S(1)}, f32[1024,256]{1,0:T(8,128)}, u32[]{:S(2)}) copy-start(f32[1024,256]{1,0:T(8,128)} %param.18) | copy-start | bytes 3145732
  7.2 9.0 %copy-start.6 = (f32[1024,256]{1,0:T(8,128)S(1)}, f32[1024,256]{1,0:T(8,128)}, u32[]{:S(2)}) copy-start(f32[1024,256]{1,0:T(8,128)} %param.19) | copy-start | bytes 3145732
  7.3 9.0 %copy-start.7 = (f32[1024,256]{1,0:T(8,128)S(1)}, f32[1024,256]{1,0:T(8,128)}, u32[]{:S(2)}) copy-start(f32[1024,256]{1,0:T(8,128)} %param.14) | copy-start | bytes 3145732
  7.3 9.0 %copy-start.8 = (f32[1024,256]{1,0:T(8,128)S(1)}, f32[1024,256]{1,0:T(8,128)}, u32[]{:S(2)}) copy-start(f32[1024,256]{1,0:T(8,128)} %param.15) | copy-start | bytes 3145732
  7.3 9.0 %copy-start.9 = (f32[1024,256]{1,0:T(8,128)S(1)}, f32[1024,256]{1,0:T(8,128)}, u32[]{:S(2)}) copy-start(f32[1024,256]{1,0:T(8,128)} %param.16) | copy-start | bytes 3145732
  17.4 19.9 %copy-start = (f32[1024,256]{1,0:T(8,128)}, f32[1024,256]{1,0:T(8,128)S(1)}, u32[]{:S(2)}) copy-start(f32[1024,256]{1,0:T(8,128)S(1)} %get-tuple-element.40) | copy-start | bytes 3145732
  17.5 19.9 %copy-start.1 = (f32[1024,256]{1,0:T(8,128)}, f32[1024,256]{1,0:T(8,128)S(1)}, u32[]{:S(2)}) copy-start(f32[1024,256]{1,0:T(8,128)S(1)} %get-tuple-element.39) | copy-start | bytes 3145732
  31.2 6.1 %copy-start.11 = (f32[256]{0:T(256)}, f32[256]{0:T(256)S(1)}, u32[]{:S(2)}) copy-start(f32[256]{0:T(256)S(1)} %sqrt.21) | copy-start | bytes 3076
  32.1 90.8 %all-gather.9.cloned.1.call-start = ((), (), s32[]{:S(2)}) async-start(), calls=%async_computation.2 | async-start | bytes 2621440 | tf_op jit(solution)/shard_map/all_gather | solution.py:52
  32.2 5.1 %copy-start.12 = (f32[256]{0:T(256)}, f32[256]{0:T(256)S(1)}, u32[]{:S(2)}) copy-start(f32[256]{0:T(256)S(1)} %sqrt.23) | copy-start | bytes 3076
  33.1 240.4 %all-gather.5.cloned.1.call-start = ((), (), s32[]{:S(2)}) async-start(), calls=%async_computation | async-start | bytes 10485760 | tf_op jit(solution)/shard_map/all_gather | solution.py:50
  33.2 4.2 %copy-start.10 = (f32[1024]{0:T(1024)}, f32[1024]{0:T(1024)S(1)}, u32[]{:S(2)}) copy-start(f32[1024]{0:T(1024)S(1)} %sqrt.19) | copy-start | bytes 12292
  33.2 4.2 %copy-start.13 = (f32[256]{0:T(256)S(1)}, f32[256]{0:T(256)}, u32[]{:S(2)}) copy-start(f32[256]{0:T(256)} %param.20) | copy-start | bytes 3076
  33.2 4.2 %copy-start.14 = (f32[256]{0:T(256)S(1)}, f32[256]{0:T(256)}, u32[]{:S(2)}) copy-start(f32[256]{0:T(256)} %param.21) | copy-start | bytes 3076
  273.5 7.9 %copy-start.2 = (bf16[4096,256]{1,0:T(8,128)(2,1)S(1)}, bf16[4096,256]{1,0:T(8,128)(2,1)}, u32[]{:S(2)}) copy-start(bf16[4096,256]{1,0:T(8,128)(2,1)} %all-gather.7.cloned.1.call-done) | copy-start | bytes 6291460
  281.4 2.3 copy-start.3
Sparse Core Ops, SparseCore 0:
  32.2 43.9 all-gather.6
  78.4 44.4 all-gather.8
  125.1 148.4 all-gather.4
where the time goes:
time: 292 us
  waiting for transfers between devices  197 us (67%)
  blocking collectives  52.6 us (18%)
  other arithmetic  16 us (5%)
  between operations  14 us (5%)
  local copies, waits for them, and re-layouts  12.3 us (4%)
    all_gather x1, waiting for transfers between devices, per_device(): lax.all_gather(narrow_query, 'rows', axis=0, tiled=True)  151 us
    all_gather x1, waiting for transfers between devices, per_device(): lax.all_gather(narrow_value, 'rows', axis=0, tiled=True)  46 us
    all_gather x1, blocking collectives, per_device(): lax.all_gather((norm_train + norm_step).astype(jnp.bfloat16), ('rows', 'w...  38.9 us
    psum x1, blocking collectives, per_device(): lax.psum((jnp.sum(result_query * result_query, axis=0), jnp.sum(result_ke...  13.7 us
    unnamed x35, local copies, waits for them, and re-layouts  12.3 us
    reduce_sum x1, other arithmetic, per_device(): jnp.sum(result_query * result_query, axis=0)  8.99 us
  transfers between devices with their start and end apart: 3, of which 2 were waited for; matrix products, arithmetic and copies ran while one was open for 2% of the time, Pallas kernels for 0%

commit v1 on v0

v1 whole, which is shorter than its diff:
```python
import functools

import jax
import jax.numpy as jnp
from jax import lax
from jax.experimental import pallas as pl
from jax.experimental.pallas import tpu as pltpu
from jax.sharding import PartitionSpec as P

learn_rate = 0.02
decay_rate = 0.05
tiny_value = 1e-08

LAG = 3
MESH = pl.DeviceIdType.MESH


def chunks_of(widths):
    out = []
    for a, width in enumerate(widths):
        step = 128 if width % 128 == 0 else width
        out += [(a, c, step) for c in range(0, width, step)]
    return out


def kernel(n, wide, chunks, *refs):
    inputs, norm_in = [refs[0:3], refs[3:6], refs[6:9]], refs[9]
    finals, columns, serve, results = refs[10:13], refs[13:16], refs[16], refs[17:20]
    held = [refs[20:23], refs[23:26], refs[26:29]]
    sums, in_sem, sum_send, sum_recv, send, recv, norm_send, norm_recv = refs[29:]
    me, col = lax.axis_index("rows"), lax.axis_index("width")
    flat, group = me * wide + col, n * wide
    depth = results[0].shape[0]
    block = min(depth, 64)

    barrier = pltpu.get_barrier_semaphore()

    def greet(p, carry):
        peer = lax.rem(flat + p, group)
        pl.semaphore_signal(
            barrier, inc=1,
            device_id={"rows": lax.div(peer, wide), "width": lax.rem(peer, wide)},
            device_id_type=MESH,
        )
        return carry

    def load(j, k):
        a, c, cw = chunks[j]
        return pltpu.make_async_copy(
            inputs[a][k].at[:, pl.ds(c, cw)], held[a][k].at[:, pl.ds(c, cw)], in_sem.at[j, k]
        )

    for j in range(len(chunks)):
        for k in range(3):
            load(j, k).start()
    lax.fori_loop(1, group, greet, 0)
    serve[flat] = norm_in[...]

    def update(j):
        a, c, cw = chunks[j]
        for k in range(3):
            load(j, k).wait()
        weight, moment, square = held[a]
        cols = pl.ds(c, cw)

        def body(i, acc):
            rows = pl.ds(pl.multiple_of(i * block, block), block)
            w = weight[rows, cols]
            r = w - learn_rate * (
                moment[rows, cols] / (jnp.sqrt(square[rows, cols]) + tiny_value) + decay_rate * w
            )
            results[a][rows, cols] = r
            return acc + jnp.sum((r * r).reshape(block // 8, 8, cw), axis=0)

        acc = lax.fori_loop(0, depth // block, body, jnp.zeros((8, cw), jnp.float32))
        sums[j, me, :, pl.ds(0, cw)] = jnp.sum(acc, axis=0, keepdims=True)

    def sum_copy(j, p, slot):
        return pltpu.make_async_remote_copy(
            src_ref=sums.at[j, me], dst_ref=sums.at[j, slot],
            send_sem=sum_send.at[j, p], recv_sem=sum_recv.at[j, p],
            device_id={"rows": lax.rem(me + p, n)}, device_id_type=MESH,
        )

    def norm_copy(p, slot):
        peer = lax.rem(flat + p, group)
        return pltpu.make_async_remote_copy(
            src_ref=serve.at[flat], dst_ref=serve.at[slot],
            send_sem=norm_send.at[p], recv_sem=norm_recv.at[p],
            device_id={"rows": lax.div(peer, wide), "width": lax.rem(peer, wide)},
            device_id_type=MESH,
        )

    has_next = (me < n - 1, me > 0)
    step = (1, -1)

    def pass_on(d, h, j, a, cols, origin):
        rows = pl.ds(pl.multiple_of(origin * depth, depth), depth)
        return pltpu.make_async_remote_copy(
            src_ref=finals[a].at[rows, cols], dst_ref=finals[a].at[rows, cols],
            send_sem=send.at[d, h, j], recv_sem=recv.at[d, h, j],
            device_id={"rows": lax.rem(me + step[d] + n, n)}, device_id_type=MESH,
        )

    def finish(j):
        a, c, cw = chunks[j]
        cols = pl.ds(c, cw)
        for p in range(1, n):
            sum_copy(j, p, lax.rem(me - p + n, n)).wait_recv()
        total = sums[j, 0, :, pl.ds(0, cw)]
        for p in range(1, n):
            total = total + sums[j, p, :, pl.ds(0, cw)]
        scale = jnp.sqrt(total)
        columns[a][:, cols] = scale
        inverse = 1.0 / scale

        def body(i, carry):
            rows = pl.ds(pl.multiple_of(i * block, block), block)
            mine = pl.ds(pl.multiple_of(me * depth + i * block, block), block)
            finals[a][mine, cols] = (results[a][rows, cols] * inverse).astype(jnp.bfloat16)
            return carry

        lax.fori_loop(0, depth // block, body, 0)
        for d in (0, 1):
            @pl.when(has_next[d])
            def _(d=d):
                pass_on(d, 0, j, a, cols, me).start()

    for j in range(len(chunks) + LAG):
        if j < len(chunks):
            update(j)
            if j == 0:
                pl.semaphore_wait(barrier, group - 1)
            for p in range(1, n):
                sum_copy(j, p, me).start()
        if j >= LAG:
            finish(j - LAG)

    def send_norm(p, carry):
        norm_copy(p, flat).start()
        return carry

    lax.fori_loop(1, group, send_norm, 0)

    counts = [sum(1 for ch in chunks if ch[0] == a) for a in range(3)]
    bases = [sum(counts[:a]) for a in range(3)]

    def each(visit):
        for h in range(n - 1):
            for a in range(3):
                cw = chunks[bases[a]][2]

                def body(k, carry, h=h, a=a, cw=cw):
                    start = pl.multiple_of(k * cw, 128) if counts[a] > 1 else 0
                    for d in (0, 1):
                        visit(d, h, bases[a] + k, a, pl.ds(start, cw))
                    return carry

                if counts[a] > 1:
                    lax.fori_loop(0, counts[a], body, 0)
                else:
                    body(0, 0)

    def relay(d, h, j, a, cols):
        origin = me - step[d] * (h + 1)

        @pl.when((origin >= 0) & (origin < n))
        def _():
            pass_on(d, h, j, a, cols, origin).wait_recv()

            if h + 1 < n - 1:
                @pl.when(has_next[d])
                def _():
                    pass_on(d, h + 1, j, a, cols, origin).start()

    each(relay)

    def drain(d, h, j, a, cols):
        origin = me - step[d] * h

        @pl.when(has_next[d] & (origin >= 0) & (origin < n))
        def _():
            pass_on(d, h, j, a, cols, origin).wait_send()

    each(drain)
    for j in range(len(chunks)):
        for p in range(1, n):
            sum_copy(j, p, me).wait_send()

    def end_norm(p, carry):
        norm_copy(p, lax.rem(flat - p + group, group)).wait_recv()
        norm_copy(p, flat).wait_send()
        return carry

    lax.fori_loop(1, group, end_norm, 0)


def solution(mesh):
    n, wide = mesh.shape["rows"], mesh.shape["width"]

    def per_device(*args):
        arrays, (norm_train, norm_step) = args[:9], args[9:]
        depth = arrays[0].shape[0]
        widths = [arrays[3 * a].shape[1] for a in range(3)]
        chunks = chunks_of(widths)
        count = len(chunks)
        part = norm_train.shape[0]
        lanes = 128 if part % 128 == 0 else part
        narrow = (norm_train + norm_step).astype(jnp.bfloat16).reshape(part // lanes, lanes)
        group = n * wide
        vmem, dma = pltpu.VMEM, pltpu.SemaphoreType.DMA
        out_shape = (
            [vmem((n * depth, w), jnp.bfloat16) for w in widths]
            + [vmem((1, w), jnp.float32) for w in widths]
            + [vmem((group, part // lanes, lanes), jnp.bfloat16)]
            + [vmem((depth, w), jnp.float32) for w in widths]
        )
        padded = sum(-(-w // 128) * 128 for w in widths)
        outside = padded * depth * (2 * n + 4) + (1 << 20)
        outs = pl.pallas_call(
            functools.partial(kernel, n, wide, chunks),
            out_shape=out_shape,
            in_specs=[pl.BlockSpec(memory_space=pltpu.HBM)] * 9 + [pl.BlockSpec(memory_space=vmem)],
            out_specs=[pl.BlockSpec(memory_space=vmem)] * 10,
            scratch_shapes=[vmem((depth, w), jnp.float32) for w in widths for _ in range(3)]
            + [
                vmem((count, n, 1, 128), jnp.float32),
                dma((count, 3)),
                dma((count, n)),
                dma((count, n)),
                dma((2, n - 1, count)),
                dma((2, n - 1, count)),
                dma((group,)),
                dma((group,)),
            ],
            compiler_params=pltpu.CompilerParams(
                collective_id=0,
                has_side_effects=True,
                vmem_limit_bytes=60 * (1 << 20) - outside,
            ),
        )(*arrays, narrow)
        return (
            *outs[0:3],
            *(c.reshape(-1) for c in outs[3:6]),
            outs[6].reshape(-1),
            *outs[7:10],
        )

    cut = P(("site", "rows"), "width")
    return jax.shard_map(
        per_device,
        mesh=mesh,
        in_specs=(cut,) * 9 + (P(("site", "rows", "width")),) * 2,
        out_specs=(P("site", "width"),) * 3
        + (P(("site", "width")),) * 3
        + (P("site"),)
        + (cut,) * 3,
        check_vma=False,
    )
```

time: 292 us -> 231 us (0.79)
  Pallas kernels: 0 us -> 217 us
  waiting for transfers between devices: 197 us -> 0 us
  blocking collectives: 52.6 us -> 0 us
  other arithmetic: 16 us -> 1.21 us
  between operations: 14 us -> 0.66 us
    pallas_call x0 -> x1, Pallas kernels: none -> 217 us  [per_device(): pl.pallas_call(functools.partial(kernel, n, wide, chunks), out_shape=out_...]
    all_gather x3 -> x0, waiting for transfers between devices: 197 us -> none  [the longest x1 151 us: per_device(): lax.all_gather(narrow_query, 'rows', axis=0, tiled=True)]
    all_gather x1 -> x0, blocking collectives: 38.9 us -> none  [per_device(): lax.all_gather((norm_train + norm_step).astype(jnp.bfloat16), ('rows', 'w...]
    psum x1 -> x0, blocking collectives: 13.7 us -> none  [per_device(): lax.psum((jnp.sum(result_query * result_query, axis=0), jnp.sum(result_ke...]
    reduce_sum x2 -> x0, other arithmetic: 10.1 us -> none  [the longest x1 8.99 us: per_device(): jnp.sum(result_query * result_query, axis=0)]
    convert_element_type x4 -> x0, other arithmetic: 5.87 us -> none  [the longest x1 4.11 us: per_device(): (result_query / column_query).astype(jnp.bfloat16)]
    unnamed x35 -> x10, local copies, waits for them, and re-layouts: 12.3 us -> 12.3 us
  transfers between devices with their start and end apart: 3 -> 0, of which waited for: 2 -> 0; matrix products, arithmetic and copies ran while one was open for 2% -> 0% of each run, Pallas kernels for 0% -> 0%
where the time goes in v1:
time: 231 us
  Pallas kernels  217 us (94%)
  local copies, waits for them, and re-layouts  12.3 us (5%)
    pallas_call x1, Pallas kernels, per_device(): pl.pallas_call(functools.partial(kernel, n, wide, chunks), out_shape=out_...  217 us
    unnamed x10, local copies, waits for them, and re-layouts  12.3 us

profile of v1, /device:TPU:0, one launch (start us, length us, event | category | flops | bytes accessed | tf_op | source)
XLA Modules:
  0.0 230.9 jit_solution(17668196827690176320)
XLA Ops:
  0.6 1.2 fusion.refs_9_
  1.9 216.7 %shard_map.186 = (bf16[4096,1024]{1,0:T(8,128)(2,1)S(1)}, bf16[4096,256]{1,0:T(8,128)(2,1)S(1)}, bf16[4096,256]{1,0:T(8,128)(2,1)S(1)}, f32[1,1024]{1,0:T(1,128)...) custom-call(f32[1024,1024]{1,0:T(8,128)} %refs_0_.1, ...), custom_call_target="tpu_custom_call" | custom-call | tf_op jit(solution)/shard_map/pallas_call | solution.py:220
  218.6 3.4 %copy.31 = bf16[4096,1024]{1,0:T(8,128)(2,1)} copy(bf16[4096,1024]{1,0:T(8,128)(2,1)S(1)} %get-tuple-element.30) | data formatting | bytes 16777216
  222.0 0.6 copy.35
  222.5 0.6 copy.36
  223.1 0.6 copy.34
  223.7 0.6 copy.37
  224.3 1.0 copy.39
  225.3 1.0 copy.40
  226.2 1.3 copy.32
  227.6 1.3 copy.33
  228.9 2.0 copy.38

commit v2 on v1

--- a/solution.py
+++ b/solution.py
@@ -24,10 +24,10 @@
 
 
 def kernel(n, wide, chunks, *refs):
-    inputs, norm_in = [refs[0:3], refs[3:6], refs[6:9]], refs[9]
-    finals, columns, serve, results = refs[10:13], refs[13:16], refs[16], refs[17:20]
-    held = [refs[20:23], refs[23:26], refs[26:29]]
-    sums, in_sem, sum_send, sum_recv, send, recv, norm_send, norm_recv = refs[29:]
+    inputs, norms = [refs[0:3], refs[3:6], refs[6:9]], refs[9:11]
+    finals, columns, serve, results = refs[11:14], refs[14:17], refs[17], refs[18:21]
+    held = [refs[21:24], refs[24:27], refs[27:30]]
+    gain, sums, in_sem, gain_sem, sum_send, sum_recv, send, recv, norm_send, norm_recv = refs[30:]
     me, col = lax.axis_index("rows"), lax.axis_index("width")
     flat, group = me * wide + col, n * wide
     depth = results[0].shape[0]
@@ -53,8 +53,9 @@
     for j in range(len(chunks)):
         for k in range(3):
             load(j, k).start()
+    for k in range(2):
+        pltpu.make_async_copy(norms[k], gain.at[k], gain_sem.at[k]).start()
     lax.fori_loop(1, group, greet, 0)
-    serve[flat] = norm_in[...]
 
     def update(j):
         a, c, cw = chunks[j]
@@ -136,6 +137,10 @@
         if j >= LAG:
             finish(j - LAG)
 
+    for k in range(2):
+        pltpu.make_async_copy(norms[k], gain.at[k], gain_sem.at[k]).wait()
+    serve[flat] = (gain[0] + gain[1]).astype(jnp.bfloat16)
+
     def send_norm(p, carry):
         norm_copy(p, flat).start()
         return carry
@@ -193,6 +198,25 @@
         return carry
 
     lax.fori_loop(1, group, end_norm, 0)
+
+
+def store(pieces, *refs):
+    count = len(pieces)
+    sem = refs[2 * count]
+    copies = []
+    for k, cut in enumerate(pieces):
+        rows = refs[k].shape[0] // cut
+        for i in range(cut):
+            part = pl.ds(i * rows, rows)
+            copies.append(
+                pltpu.make_async_copy(
+                    refs[k].at[part], refs[count + k].at[part], sem.at[len(copies)]
+                )
+            )
+    for copy in copies:
+        copy.start()
+    for copy in copies:
+        copy.wait()
 
 
 def solution(mesh):
@@ -206,7 +230,7 @@
         count = len(chunks)
         part = norm_train.shape[0]
         lanes = 128 if part % 128 == 0 else part
-        narrow = (norm_train + norm_step).astype(jnp.bfloat16).reshape(part // lanes, lanes)
+        norms = [x.reshape(part // lanes, lanes) for x in (norm_train, norm_step)]
         group = n * wide
         vmem, dma = pltpu.VMEM, pltpu.SemaphoreType.DMA
         out_shape = (
@@ -220,12 +244,14 @@
         outs = pl.pallas_call(
             functools.partial(kernel, n, wide, chunks),
             out_shape=out_shape,
-            in_specs=[pl.BlockSpec(memory_space=pltpu.HBM)] * 9 + [pl.BlockSpec(memory_space=vmem)],
+            in_specs=[pl.BlockSpec(memory_space=pltpu.HBM)] * 11,
             out_specs=[pl.BlockSpec(memory_space=vmem)] * 10,
             scratch_shapes=[vmem((depth, w), jnp.float32) for w in widths for _ in range(3)]
             + [
+                vmem((2, part // lanes, lanes), jnp.float32),
                 vmem((count, n, 1, 128), jnp.float32),
                 dma((count, 3)),
+                dma((2,)),
                 dma((count, n)),
                 dma((count, n)),
                 dma((2, n - 1, count)),
@@ -238,7 +264,16 @@
                 has_side_effects=True,
                 vmem_limit_bytes=60 * (1 << 20) - outside,
             ),
-        )(*arrays, narrow)
+        )(*arrays, *norms)
+        pieces = [n, 1, 1, 1, 1, 1, 1, 2, 1, 1]
+        outs = pl.pallas_call(
+            functools.partial(store, pieces),
+            out_shape=[jax.ShapeDtypeStruct(x.shape, x.dtype) for x in outs],
+            in_specs=[pl.BlockSpec(memory_space=vmem)] * 10,
+            out_specs=[pl.BlockSpec(memory_space=pltpu.HBM)] * 10,
+            scratch_shapes=[dma((sum(pieces),))],
+            compiler_params=pltpu.CompilerParams(vmem_limit_bytes=1 << 20),
+        )(*(pltpu.with_memory_space_constraint(x, vmem) for x in outs))
         return (
             *outs[0:3],
             *(c.reshape(-1) for c in outs[3:6]),

time: 231 us -> 224 us (0.970)
  local copies, waits for them, and re-layouts: 12.3 us -> 0 us
  Pallas kernels: 217 us -> 223 us
    unnamed x10 -> x0, local copies, waits for them, and re-layouts: 12.3 us -> none
    pallas_call x0 -> x1, Pallas kernels: none -> 6.6 us  [per_device(): pl.pallas_call(functools.partial(store, pieces), out_shape=[jax.ShapeDtyp...]
where the time goes in v2:
time: 224 us; the launch traced here: 223 us
  Pallas kernels  223 us (100%)
    pallas_call x1, Pallas kernels, per_device(): pl.pallas_call(functools.partial(kernel, n, wide, chunks), out_shape=out_...  216 us
    pallas_call x1, Pallas kernels, per_device(): pl.pallas_call(functools.partial(store, pieces), out_shape=[jax.ShapeDtyp...  6.6 us

profile of v2, /device:TPU:0, one launch (start us, length us, event | category | flops | bytes accessed | tf_op | source)
XLA Modules:
  0.0 223.4 jit_solution(1116289301412440331)
XLA Ops:
  0.6 216.2 %shard_map.186 = (bf16[4096,1024]{1,0:T(8,128)(2,1)S(1)}, bf16[4096,256]{1,0:T(8,128)(2,1)S(1)}, bf16[4096,256]{1,0:T(8,128)(2,1)S(1)}, f32[1,1024]{1,0:T(1,128)...) custom-call(f32[1024,1024]{1,0:T(8,128)} %refs_0_.1, ...), custom_call_target="tpu_custom_call" | custom-call | tf_op jit(solution)/shard_map/pallas_call | solution.py:244
  216.8 6.6 %shard_map.187 = (bf16[4096,1024]{1,0:T(8,128)(2,1)}, bf16[4096,256]{1,0:T(8,128)(2,1)}, bf16[4096,256]{1,0:T(8,128)(2,1)}, f32[1,1024]{1,0:T(1,128)}, f32[1,256...) custom-call(bf16[4096,1024]{1,0:T(8,128)(2,1)S(1)} %get-tuple-elemen, ...), custom_call_target="tpu_custom_call" | custom-call | tf_op jit(solution)/shard_map/pallas_call | solution.py:269

commit v3 on v2

--- a/solution.py
+++ b/solution.py
@@ -11,7 +11,7 @@
 decay_rate = 0.05
 tiny_value = 1e-08
 
-LAG = 3
+LAG = 1
 MESH = pl.DeviceIdType.MESH
 
 
@@ -50,7 +50,8 @@
             inputs[a][k].at[:, pl.ds(c, cw)], held[a][k].at[:, pl.ds(c, cw)], in_sem.at[j, k]
         )
 
-    for j in range(len(chunks)):
+    ahead = min(2, len(chunks))
+    for j in range(ahead):
         for k in range(3):
             load(j, k).start()
     for k in range(2):
@@ -61,6 +62,9 @@
         a, c, cw = chunks[j]
         for k in range(3):
             load(j, k).wait()
+        if j + ahead < len(chunks):
+            for k in range(3):
+                load(j + ahead, k).start()
         weight, moment, square = held[a]
         cols = pl.ds(c, cw)
 

time: 224 us -> 224 us (level)
  no operation moved by 1% of the time
where the time goes in v3:
time: 224 us; the launch traced here: 223 us
  Pallas kernels  223 us (100%)
    pallas_call x1, Pallas kernels, per_device(): pl.pallas_call(functools.partial(kernel, n, wide, chunks), out_shape=out_...  216 us
    pallas_call x1, Pallas kernels, per_device(): pl.pallas_call(functools.partial(store, pieces), out_shape=[jax.ShapeDtyp...  6.6 us

profile of v3, /device:TPU:0, one launch (start us, length us, event | category | flops | bytes accessed | tf_op | source)
XLA Modules:
  0.0 223.4 jit_solution(6845767069021213522)
XLA Ops:
  0.6 216.1 %shard_map.186 = (bf16[4096,1024]{1,0:T(8,128)(2,1)S(1)}, bf16[4096,256]{1,0:T(8,128)(2,1)S(1)}, bf16[4096,256]{1,0:T(8,128)(2,1)S(1)}, f32[1,1024]{1,0:T(1,128)...) custom-call(f32[1024,1024]{1,0:T(8,128)} %refs_0_.1, ...), custom_call_target="tpu_custom_call" | custom-call | tf_op jit(solution)/shard_map/pallas_call | solution.py:248
  216.8 6.6 %shard_map.187 = (bf16[4096,1024]{1,0:T(8,128)(2,1)}, bf16[4096,256]{1,0:T(8,128)(2,1)}, bf16[4096,256]{1,0:T(8,128)(2,1)}, f32[1,1024]{1,0:T(1,128)}, f32[1,256...) custom-call(bf16[4096,1024]{1,0:T(8,128)(2,1)S(1)} %get-tuple-elemen, ...), custom_call_target="tpu_custom_call" | custom-call | tf_op jit(solution)/shard_map/pallas_call | solution.py:273
